TPU v7x, 32 devices: a whole 2x2x4 slice. The times are simulated.
32 devices in a mesh: vocab: 8 (over y, x, core), hid: 4 (over z).
Axes of the slice: x: 2, y: 2, z: 4, core: 2. Of those that a mesh axis runs over, the one named last changes fastest.
Arguments:
- hidden: bfloat16 [2, 256, 7168], P(None, 'vocab', 'hid'), may hold values from -100 to 100
- head_weight: bfloat16 [7168, 65536], P('hid', 'vocab'), may hold values from -2 to 2
- targets: int32 [2, 256], P(None, 'hid'), may hold values from 0 to 65535
Outputs:
- entropy: float32 [2, 256], P(None, 'hid')
- squared: float32 [2, 256], P(None, 'hid')
All inputs are finite; a program needn't handle non-finite values.
Results may differ from a plain program's by a relative error of at most 0.0003.
Values may be sent and summed in bfloat16 or wider, within the bound.
A program may use at most 192 MiB of HBM per device.

v0:
```python
import functools

import jax
import jax.numpy as jnp
from jax import lax
from jax.experimental import pallas as pl
from jax.experimental.pallas import tpu as pltpu
from jax.sharding import PartitionSpec as P

MESH = pl.DeviceIdType.MESH
LANES = 128
SKEW = 3
AHEAD = 3
LOWEST = -3.0e38
TOP = 32767.0


def kernel(
    n, nv, nj, cw, ring,
    hidden, weight, targets,
    out,
    rows, wbuf, came, gone, came_scale, gone_scale, part,
    labels, label_tile, peak, mass, pick, ends, mine, shared,
    w_sem, own_sem, h_send, h_recv, l_send, l_recv,
    q_send, q_recv, s_send, s_recv, e_send, e_recv, c_send, c_recv,
):
    v, me = lax.axis_index("vocab"), lax.axis_index("hid")
    groups = nv // 2
    chip, parity = v // 2, v % 2
    depths, share, width = hidden.shape
    block = depths * share
    half = nj * cw
    span = 2 * nj
    units = nv * nj
    columns = [slice(c * LANES, (c + 1) * LANES) for c in range(cw // LANES)]
    low = me < n // 2
    ways = (jnp.where(low, 0, 1), jnp.where(low, 1, 0))
    near = jnp.where(low, me, n - 1 - me)
    places = (near, n - 1 - near)
    nexts = (jnp.where(low, me + 1, me - 1), jnp.where(low, me - 1, me + 1))

    def w_copy(t, j):
        return pltpu.make_async_copy(
            weight.at[:, pl.ds(pl.multiple_of(ways[t] * half + j * cw, cw), cw)],
            wbuf.at[ways[t] * nj + j],
            w_sem.at[t * nj + j],
        )

    own = pltpu.make_async_copy(hidden, rows.at[chip, parity], own_sem)
    own.start()
    w_copy(0, 0).start()

    barrier = pltpu.get_barrier_semaphore()
    for k in range(1, nv):
        pl.semaphore_signal(barrier, inc=1, device_id=((v + k) % nv, me), device_id_type=MESH)
    for k in range(1, n):
        pl.semaphore_signal(barrier, inc=1, device_id=(v, (me + k) % n), device_id_type=MESH)

    for j in range(1, AHEAD):
        w_copy(0, j).start()
    for j in range(AHEAD - 1):
        w_copy(1, j).start()

    def h_copy(target):
        return pltpu.make_async_remote_copy(
            src_ref=hidden, dst_ref=rows.at[chip, parity], send_sem=h_send, recv_sem=h_recv.at[v],
            device_id=(target, me), device_id_type=MESH,
        )

    def h_arrival(g, side):
        return pltpu.make_async_remote_copy(
            src_ref=hidden, dst_ref=rows.at[g, side], send_sem=h_send, recv_sem=h_recv.at[2 * g + side],
            device_id=(v, me), device_id_type=MESH,
        )

    def small_dot(t, u):
        j = u % nj
        a = rows[chip, (v + u // nj) % 2].reshape(block, width)
        part[t, u % 2] = jnp.dot(a, wbuf[ways[t] * nj + j], preferred_element_type=jnp.float32)

    def group_of(u):
        return (chip + u // span) % groups

    def dot(t, u):
        @pl.when(u < span)
        def _():
            @pl.when(u < nj)
            def _():
                @pl.when(u + AHEAD - 1 < nj)
                def _():
                    w_copy(t, u + AHEAD - 1).start()

                w_copy(t, u).wait()

            if t == 0:
                @pl.when(u == nj)
                def _():
                    h_arrival(chip, 1 - parity).wait_recv()

            small_dot(t, u)

        @pl.when(jnp.logical_and(jnp.logical_and(u >= span, u < units), u % 2 == 0))
        def _():
            g = group_of(u)
            if t == 0:
                @pl.when(u % span == 0)
                def _():
                    for side in range(2):
                        h_arrival(g, side).wait_recv()

            a = rows[g].reshape(2 * block, width)
            y = jnp.dot(a, wbuf[ways[t] * nj + (u % span) // 2], preferred_element_type=jnp.float32)
            part[t] = y.reshape(2, block, cw)

    own.wait()
    w_copy(0, 0).wait()
    small_dot(0, 0)
    pl.semaphore_wait(barrier, nv - 1 + n - 1)

    peers = [2 * chip + 1 - parity]
    for back in range(1, groups):
        other = (chip - back + groups) % groups
        peers += [2 * other + parity, 2 * other + 1 - parity]
    for target in peers:
        h_copy(target).start()

    finals = (n - 1, 0)

    def l_copy(e):
        return pltpu.make_async_remote_copy(
            src_ref=targets, dst_ref=labels.at[me], send_sem=l_send.at[e], recv_sem=l_recv.at[me],
            device_id=(v, finals[e]), device_id_type=MESH,
        )

    for e in range(2):
        @pl.when(me != finals[e])
        def _():
            l_copy(e).start()

        @pl.when(me == finals[e])
        def _():
            labels[me] = targets[...]

    def message(t, u, target):
        way = ways[t]
        data = pltpu.make_async_remote_copy(
            src_ref=gone.at[way, u], dst_ref=came.at[way, u],
            send_sem=q_send.at[way], recv_sem=q_recv.at[way, u % ring],
            device_id=(v, target), device_id_type=MESH,
        )
        scale = pltpu.make_async_remote_copy(
            src_ref=gone_scale.at[way, u], dst_ref=came_scale.at[way, u],
            send_sem=s_send.at[way], recv_sem=s_recv.at[way, u % ring],
            device_id=(v, target), device_id_type=MESH,
        )
        return scale, data

    def send_end(e, g):
        return pltpu.make_async_remote_copy(
            src_ref=ends.at[g], dst_ref=mine.at[e], send_sem=e_send.at[g], recv_sem=e_recv.at[e],
            device_id=(v, g), device_id_type=MESH,
        )

    def held(t, u):
        return [part[t, u % 2, :, c] for c in columns]

    def received(t, u):
        for copy in message(t, u, me):
            copy.wait_recv()
        scale = came_scale[ways[t], u]
        return [
            part[t, u % 2, :, c] + came[ways[t], u, :, c].astype(jnp.int32).astype(jnp.float32) * scale
            for c in columns
        ]

    def ship(t, u, pieces):
        largest = functools.reduce(jnp.maximum, [jnp.abs(piece) for piece in pieces])
        largest = jnp.maximum(jnp.max(largest, axis=0, keepdims=True), 1e-30)
        gone_scale[ways[t], u] = largest * (1.0 / TOP)
        up = TOP / largest
        for c, piece in zip(columns, pieces):
            gone[ways[t], u, :, c] = jnp.round(piece * up).astype(jnp.int32).astype(jnp.int16)
        for copy in message(t, u, nexts[t]):
            copy.start()

    def order(line):
        return jnp.concatenate(
            [line[a : a + 1, s * share : (s + 1) * share] for s in range(2) for a in range(depths)], axis=1
        )

    def statistics(u, pieces):
        g, r = group_of(u), u % span

        @pl.when(u == 0)
        def _():
            for z in range(n):
                @pl.when(me != z)
                def _():
                    pltpu.make_async_remote_copy(
                        src_ref=targets, dst_ref=labels.at[z], send_sem=l_send.at[0], recv_sem=l_recv.at[z],
                        device_id=(v, me), device_id_type=MESH,
                    ).wait_recv()

        @pl.when(r == 0)
        def _():
            label_tile[...] = jnp.transpose(jnp.broadcast_to(order(labels[g]), (LANES, 2 * block)))
            peak[...] = jnp.full_like(peak, LOWEST)
            mass[...] = jnp.zeros_like(mass)
            pick[...] = jnp.zeros_like(pick)

        first_group = u < span
        side = jnp.where(first_group, (v + u // nj) % 2, r % 2)
        j = jnp.where(first_group, u % nj, r // 2)
        here = pl.ds(pl.multiple_of(side * block, block), block)
        old = peak[here, :]
        new = functools.reduce(jnp.maximum, pieces, old)
        peak[here, :] = new
        mass[here, :] = mass[here, :] * jnp.exp(old - new) + sum(jnp.exp(piece - new) for piece in pieces)
        offset = label_tile[here, :] - (v * (2 * half) + ways[1] * half + j * cw)
        lane = lax.broadcasted_iota(jnp.int32, (block, LANES), 1)
        found = pick[here, :]
        for c, piece in enumerate(pieces):
            found = found + jnp.where(offset == lane + c * LANES, piece, 0.0)
        pick[here, :] = found

        @pl.when(r == span - 1)
        def _():
            tall = jnp.transpose(peak[...])
            top = jnp.max(tall, axis=0, keepdims=True)
            weight_sum = jnp.sum(jnp.transpose(mass[...]) * jnp.exp(tall - top), axis=0, keepdims=True)
            chosen = jnp.sum(jnp.transpose(pick[...]), axis=0, keepdims=True)
            ends[g] = jnp.concatenate(
                [top, weight_sum, chosen, jnp.zeros((5, 2 * block), jnp.float32)], axis=0
            )

            @pl.when(g != me)
            def _():
                send_end(ways[1], g).start()

            @pl.when(g == me)
            def _():
                mine[ways[1]] = ends[g]

    def step(i, carry):
        u = i - places[0] * SKEW

        @pl.when(jnp.logical_and(u >= 0, u < units))
        def _():
            @pl.when(places[0] == 0)
            def _():
                ship(0, u, held(0, u))

            @pl.when(places[0] > 0)
            def _():
                ship(0, u, received(0, u))

            dot(0, u + 1)

        w = i - places[1] * SKEW

        @pl.when(jnp.logical_and(w >= 0, w < units))
        def _():
            @pl.when(places[1] < n - 1)
            def _():
                ship(1, w, received(1, w))

            @pl.when(places[1] == n - 1)
            def _():
                statistics(w, received(1, w))

        @pl.when(jnp.logical_and(w >= -1, w < units))
        def _():
            dot(1, w + 1)

        return carry

    lax.fori_loop(0, units + (n - 1) * SKEW, step, 0)

    for e in range(2):
        @pl.when(me != finals[e])
        def _():
            send_end(e, me).wait_recv()

    def merge(tiles):
        top = functools.reduce(jnp.maximum, [t[0:1] for t in tiles])
        weight_sum = sum(t[1:2] * jnp.exp(t[0:1] - top) for t in tiles)
        chosen = sum(t[2:3] for t in tiles)
        return top, weight_sum, chosen

    top, weight_sum, chosen = merge([mine[0], mine[1]])
    shared[v] = jnp.concatenate([top, weight_sum, chosen, jnp.zeros((5, 2 * block), jnp.float32)], axis=0)

    def c_copy(slot, source, target):
        return pltpu.make_async_remote_copy(
            src_ref=shared.at[source], dst_ref=shared.at[source], send_sem=c_send.at[slot], recv_sem=c_recv.at[source],
            device_id=(target, me), device_id_type=MESH,
        )

    for k in range(1, nv):
        c_copy(k - 1, v, (v + k) % nv).start()

    for _ in range(nv - 1):
        h_copy(v).wait_send()
    for e in range(2):
        @pl.when(me != finals[e])
        def _():
            l_copy(e).wait_send()
    for t in range(2):
        @pl.when(places[t] < n - 1)
        def _():
            pltpu.make_async_copy(gone.at[ways[t]], came.at[ways[t]], q_send.at[ways[t]]).wait()
            pltpu.make_async_copy(gone_scale.at[ways[t]], came_scale.at[ways[t]], s_send.at[ways[t]]).wait()

    @pl.when(places[1] == n - 1)
    def _():
        for g in range(groups):
            @pl.when(me != g)
            def _():
                send_end(ways[1], g).wait_send()

    for k in range(1, nv):
        c_copy(0, (v + k) % nv, v).wait_recv()
    top, weight_sum, chosen = merge([shared[k] for k in range(nv)])
    norm = top + jnp.log(weight_sum)
    for b, line in enumerate((norm, chosen)):
        for a in range(depths):
            out[depths * b + a : depths * b + a + 1, :] = jnp.concatenate(
                [line[:, (s * depths + a) * share : (s * depths + a + 1) * share] for s in range(2)], axis=1
            )

    for k in range(1, nv):
        c_copy(k - 1, v, (v + k) % nv).wait_send()


def body(n, nv, hidden, head_weight, targets):
    depths, share, width = hidden.shape
    columns = head_weight.shape[1]
    groups = nv // 2
    assert groups == n and n >= 2 and depths * 2 * share == LANES
    cw = min(512, columns // 2)
    nj = columns // 2 // cw
    units = nv * nj
    block = depths * share
    ring = 16
    while ring < (n - 1) * SKEW + 4:
        ring *= 2
    vmem, anywhere = pl.BlockSpec(memory_space=pltpu.VMEM), pl.BlockSpec(memory_space=pl.ANY)
    dma = pltpu.SemaphoreType.DMA
    result = pl.pallas_call(
        functools.partial(kernel, n, nv, nj, cw, ring),
        out_shape=jax.ShapeDtypeStruct((2 * depths, targets.shape[1]), jnp.float32),
        in_specs=[anywhere, anywhere, vmem],
        out_specs=vmem,
        scratch_shapes=[
            pltpu.VMEM((groups, 2, depths, share, width), hidden.dtype),
            pltpu.VMEM((2 * nj, width, cw), head_weight.dtype),
            pltpu.VMEM((2, units, block, cw), jnp.int16),
            pltpu.VMEM((2, units, block, cw), jnp.int16),
            pltpu.VMEM((2, units, 1, LANES), jnp.float32),
            pltpu.VMEM((2, units, 1, LANES), jnp.float32),
            pltpu.VMEM((2, 2, block, cw), jnp.float32),
            pltpu.VMEM((n,) + targets.shape, jnp.int32),
            pltpu.VMEM((2 * block, LANES), jnp.int32),
            pltpu.VMEM((2 * block, LANES), jnp.float32),
            pltpu.VMEM((2 * block, LANES), jnp.float32),
            pltpu.VMEM((2 * block, LANES), jnp.float32),
            pltpu.VMEM((groups, 8, 2 * block), jnp.float32),
            pltpu.VMEM((2, 8, 2 * block), jnp.float32),
            pltpu.VMEM((nv, 8, 2 * block), jnp.float32),
            dma((2 * nj,)), dma, dma, dma((nv,)), dma((2,)), dma((n,)),
            dma((2,)), dma((2, ring)), dma((2,)), dma((2, ring)),
            dma((groups,)), dma((2,)), dma((nv - 1,)), dma((nv,)),
        ],
        compiler_params=pltpu.CompilerParams(
            collective_id=0, has_side_effects=True, vmem_limit_bytes=60 * 1024 * 1024
        ),
    )(hidden, head_weight, targets)
    norm, chosen = result[:depths], result[depths:]
    return norm - chosen, norm * norm


def solution(mesh):
    return jax.shard_map(
        functools.partial(body, mesh.shape["hid"], mesh.shape["vocab"]),
        mesh=mesh,
        in_specs=(P(None, "vocab", "hid"), P("hid", "vocab"), P(None, "hid")),
        out_specs=(P(None, "hid"), P(None, "hid")),
        check_vma=False,
    )
```

profile of v0, /device:TPU:0, one launch (start us, length us, event | category | flops | bytes accessed | tf_op | source)
XLA Modules:
  0.0 117.4 jit_solution(10266067133856583117)
XLA Ops:
  0.6 115.5 %shard_map.50 = f32[4,64]{1,0:T(4,128)} custom-call(bf16[2,32,1792]{2,1,0:T(8,128)(2,1)} %hidden.1, bf16[1792,8192]{1,0:T(8,128)(2,1)} %weight.1, s32[2,64]{1,0:T(2,128)} %targets.1), custom_call_target="tpu_custom_call" | custom-call | tf_op jit(solution)/shard_map/pallas_call | solution.py:349
  116.1 1.3 %slice_multiply_fusion = (f32[2,64]{1,0:T(2,128)}, f32[2,64]{1,0:T(2,128)}) fusion(f32[4,64]{1,0:T(4,128)} %shard_map.50), kind=kLoop, calls=%fused_computation.1 | loop fusion | flops 256 | bytes 2048 | tf_op jit(solution)/shard_map/mul | solution.py:379
where the time goes:
time: 118 us; the launch traced here: 117 us
  Pallas kernels  115 us (97%)
  other arithmetic  1.32 us (1%)
    pallas_call x1, Pallas kernels, body(): pl.pallas_call(functools.partial(kernel, n, nv, nj, cw, ring), out_shape=...  115 us

commit v1 on v0

--- a/solution.py
+++ b/solution.py
@@ -11,6 +11,7 @@
 LANES = 128
 SKEW = 3
 AHEAD = 3
+BACK = 2
 LOWEST = -3.0e38
 TOP = 32767.0
 
@@ -20,9 +21,9 @@
     hidden, weight, targets,
     out,
     rows, wbuf, came, gone, came_scale, gone_scale, part,
-    labels, label_tile, peak, mass, pick, ends, mine, shared,
+    labels, label_tile, peak, mass, pick, ends, mine, shared, late,
     w_sem, own_sem, h_send, h_recv, l_send, l_recv,
-    q_send, q_recv, s_send, s_recv, e_send, e_recv, c_send, c_recv,
+    q_send, q_recv, s_send, s_recv, e_send, e_recv, c_send, c_recv, t_send, t_recv,
 ):
     v, me = lax.axis_index("vocab"), lax.axis_index("hid")
     groups = nv // 2
@@ -39,6 +40,12 @@
     places = (near, n - 1 - near)
     nexts = (jnp.where(low, me + 1, me - 1), jnp.where(low, me - 1, me + 1))
 
+    kept = units - BACK
+    ending = (0, 1, n - 2, n - 1)
+
+    def last_group(c):
+        return n // 2 - 1 + c % 2
+
     def w_copy(t, j):
         return pltpu.make_async_copy(
             weight.at[:, pl.ds(pl.multiple_of(ways[t] * half + j * cw, cw), cw)],
@@ -49,6 +56,12 @@
     own = pltpu.make_async_copy(hidden, rows.at[chip, parity], own_sem)
     own.start()
     w_copy(0, 0).start()
+    row = lax.broadcasted_iota(jnp.int32, (8, 2 * block), 0)
+    neutral = jnp.where(row == 0, LOWEST, 0.0)
+    for k in range(nv):
+        shared[k] = neutral
+        for e in range(len(ending)):
+            late[k, e] = neutral
 
     barrier = pltpu.get_barrier_semaphore()
     for k in range(1, nv):
@@ -79,7 +92,15 @@
         part[t, u % 2] = jnp.dot(a, wbuf[ways[t] * nj + j], preferred_element_type=jnp.float32)
 
     def group_of(u):
-        return (chip + u // span) % groups
+        turn = u // span
+        natural, final = (chip + turn) % groups, last_group(chip)
+        other = jnp.where(natural == final, (chip + groups - 1) % groups, natural)
+        return jnp.where(turn == groups - 1, final, other)
+
+    def big_dot(t, g, chunk):
+        a = rows[g].reshape(2 * block, width)
+        y = jnp.dot(a, wbuf[chunk], preferred_element_type=jnp.float32)
+        part[t] = y.reshape(2, block, cw)
 
     def dot(t, u):
         @pl.when(u < span)
@@ -108,9 +129,12 @@
                     for side in range(2):
                         h_arrival(g, side).wait_recv()
 
-            a = rows[g].reshape(2 * block, width)
-            y = jnp.dot(a, wbuf[ways[t] * nj + (u % span) // 2], preferred_element_type=jnp.float32)
-            part[t] = y.reshape(2, block, cw)
+            big_dot(t, g, ways[t] * nj + (u % span) // 2)
+
+        if t == 0:
+            @pl.when(jnp.logical_and(u == units, places[0] == 0))
+            def _():
+                big_dot(0, last_group(chip), ways[1] * nj + nj - 1)
 
     own.wait()
     w_copy(0, 0).wait()
@@ -129,15 +153,15 @@
     def l_copy(e):
         return pltpu.make_async_remote_copy(
             src_ref=targets, dst_ref=labels.at[me], send_sem=l_send.at[e], recv_sem=l_recv.at[me],
-            device_id=(v, finals[e]), device_id_type=MESH,
-        )
-
-    for e in range(2):
-        @pl.when(me != finals[e])
+            device_id=(v, ending[e]), device_id_type=MESH,
+        )
+
+    for e in range(len(ending)):
+        @pl.when(me != ending[e])
         def _():
             l_copy(e).start()
 
-        @pl.when(me == finals[e])
+        @pl.when(me == ending[e])
         def _():
             labels[me] = targets[...]
 
@@ -172,6 +196,24 @@
             part[t, u % 2, :, c] + came[ways[t], u, :, c].astype(jnp.int32).astype(jnp.float32) * scale
             for c in columns
         ]
+
+    def returned(u):
+        for copy in message(0, u, me):
+            copy.wait_recv()
+        scale = came_scale[ways[0], u]
+        return [came[ways[0], u, :, c].astype(jnp.int32).astype(jnp.float32) * scale for c in columns]
+
+    def late_copy(e, target):
+        return pltpu.make_async_remote_copy(
+            src_ref=ends.at[last_group(chip)], dst_ref=late.at[v, e], send_sem=t_send, recv_sem=t_recv.at[v, e],
+            device_id=(target, last_group(chip)), device_id_type=MESH,
+        )
+
+    def late_arrival(k, e):
+        return pltpu.make_async_remote_copy(
+            src_ref=ends.at[0], dst_ref=late.at[k, e], send_sem=t_send, recv_sem=t_recv.at[k, e],
+            device_id=(v, me), device_id_type=MESH,
+        )
 
     def ship(t, u, pieces):
         largest = functools.reduce(jnp.maximum, [jnp.abs(piece) for piece in pieces])
@@ -188,10 +230,10 @@
             [line[a : a + 1, s * share : (s + 1) * share] for s in range(2) for a in range(depths)], axis=1
         )
 
-    def statistics(u, pieces):
+    def statistics(u, pieces, start, stop):
         g, r = group_of(u), u % span
 
-        @pl.when(u == 0)
+        @pl.when(u == start)
         def _():
             for z in range(n):
                 @pl.when(me != z)
@@ -201,7 +243,7 @@
                         device_id=(v, me), device_id_type=MESH,
                     ).wait_recv()
 
-        @pl.when(r == 0)
+        @pl.when(jnp.logical_or(r == 0, u == start))
         def _():
             label_tile[...] = jnp.transpose(jnp.broadcast_to(order(labels[g]), (LANES, 2 * block)))
             peak[...] = jnp.full_like(peak, LOWEST)
@@ -223,7 +265,7 @@
             found = found + jnp.where(offset == lane + c * LANES, piece, 0.0)
         pick[here, :] = found
 
-        @pl.when(r == span - 1)
+        @pl.when(jnp.logical_or(r == span - 1, u == stop - 1))
         def _():
             tall = jnp.transpose(peak[...])
             top = jnp.max(tall, axis=0, keepdims=True)
@@ -233,53 +275,70 @@
                 [top, weight_sum, chosen, jnp.zeros((5, 2 * block), jnp.float32)], axis=0
             )
 
-            @pl.when(g != me)
+            @pl.when(u == stop - 1)
+            def _():
+                for e in range(len(ending)):
+                    @pl.when(me == ending[e])
+                    def _():
+                        @pl.when(me == last_group(chip))
+                        def _():
+                            late[v, e] = ends[last_group(chip)]
+
+                        for k in range(nv):
+                            @pl.when(jnp.logical_or(me != last_group(chip), v != k))
+                            def _():
+                                late_copy(e, k).start()
+
+            @pl.when(jnp.logical_and(u != stop - 1, g != me))
             def _():
                 send_end(ways[1], g).start()
 
-            @pl.when(g == me)
+            @pl.when(jnp.logical_and(u != stop - 1, g == me))
             def _():
                 mine[ways[1]] = ends[g]
 
     def step(i, carry):
         u = i - places[0] * SKEW
+        extra = jnp.where(places[0] == 0, BACK, 0)
+
+        @pl.when(jnp.logical_and(u >= 0, u < units + extra))
+        def _():
+            @pl.when(places[0] == 0)
+            def _():
+                ship(0, u, held(0, u))
+
+            @pl.when(places[0] > 0)
+            def _():
+                ship(0, u, received(0, u))
+
+        w = i - places[1] * SKEW
+
+        @pl.when(jnp.logical_and(w >= 0, w < units))
+        def _():
+            @pl.when(jnp.logical_and(places[1] < n - 1, jnp.logical_or(w < kept, places[1] < n - 2)))
+            def _():
+                ship(1, w, received(1, w))
+
+            @pl.when(jnp.logical_and(places[1] == n - 1, w < kept))
+            def _():
+                statistics(w, received(1, w), 0, kept)
+
+            @pl.when(jnp.logical_and(places[1] == n - 2, w >= kept))
+            def _():
+                total = [a + b for a, b in zip(received(1, w), returned(w + BACK))]
+                statistics(w, total, kept, units)
 
         @pl.when(jnp.logical_and(u >= 0, u < units))
         def _():
-            @pl.when(places[0] == 0)
-            def _():
-                ship(0, u, held(0, u))
-
-            @pl.when(places[0] > 0)
-            def _():
-                ship(0, u, received(0, u))
-
             dot(0, u + 1)
 
-        w = i - places[1] * SKEW
-
-        @pl.when(jnp.logical_and(w >= 0, w < units))
-        def _():
-            @pl.when(places[1] < n - 1)
-            def _():
-                ship(1, w, received(1, w))
-
-            @pl.when(places[1] == n - 1)
-            def _():
-                statistics(w, received(1, w))
-
-        @pl.when(jnp.logical_and(w >= -1, w < units))
+        @pl.when(jnp.logical_and(w >= -1, w < jnp.where(places[1] == n - 1, kept, units) - 1))
         def _():
             dot(1, w + 1)
 
         return carry
 
     lax.fori_loop(0, units + (n - 1) * SKEW, step, 0)
-
-    for e in range(2):
-        @pl.when(me != finals[e])
-        def _():
-            send_end(e, me).wait_recv()
 
     def merge(tiles):
         top = functools.reduce(jnp.maximum, [t[0:1] for t in tiles])
@@ -287,40 +346,73 @@
         chosen = sum(t[2:3] for t in tiles)
         return top, weight_sum, chosen
 
-    top, weight_sum, chosen = merge([mine[0], mine[1]])
-    shared[v] = jnp.concatenate([top, weight_sum, chosen, jnp.zeros((5, 2 * block), jnp.float32)], axis=0)
-
     def c_copy(slot, source, target):
         return pltpu.make_async_remote_copy(
             src_ref=shared.at[source], dst_ref=shared.at[source], send_sem=c_send.at[slot], recv_sem=c_recv.at[source],
             device_id=(target, me), device_id_type=MESH,
         )
 
-    for k in range(1, nv):
-        c_copy(k - 1, v, (v + k) % nv).start()
+    early = last_group(chip) != me
+
+    @pl.when(early)
+    def _():
+        for e in range(2):
+            @pl.when(me != finals[e])
+            def _():
+                send_end(e, me).wait_recv()
+
+        top, weight_sum, chosen = merge([mine[0], mine[1]])
+        shared[v] = jnp.concatenate([top, weight_sum, chosen, jnp.zeros((5, 2 * block), jnp.float32)], axis=0)
+        for k in range(1, nv):
+            c_copy(k - 1, v, (v + k) % nv).start()
 
     for _ in range(nv - 1):
         h_copy(v).wait_send()
-    for e in range(2):
-        @pl.when(me != finals[e])
+    for e in range(len(ending)):
+        @pl.when(me != ending[e])
         def _():
             l_copy(e).wait_send()
-    for t in range(2):
-        @pl.when(places[t] < n - 1)
-        def _():
-            pltpu.make_async_copy(gone.at[ways[t]], came.at[ways[t]], q_send.at[ways[t]]).wait()
-            pltpu.make_async_copy(gone_scale.at[ways[t]], came_scale.at[ways[t]], s_send.at[ways[t]]).wait()
+
+    def sent(t, count):
+        way = ways[t]
+        pltpu.make_async_copy(gone.at[way, 0:count], came.at[way, 0:count], q_send.at[way]).wait()
+        pltpu.make_async_copy(gone_scale.at[way, 0:count], came_scale.at[way, 0:count], s_send.at[way]).wait()
+
+    for t, role, count in (
+        (0, places[0] == 0, units + BACK), (0, places[0] > 0, units),
+        (1, places[1] < n - 2, units), (1, places[1] == n - 2, kept),
+    ):
+        @pl.when(role)
+        def _():
+            sent(t, count)
 
     @pl.when(places[1] == n - 1)
     def _():
         for g in range(groups):
-            @pl.when(me != g)
+            @pl.when(jnp.logical_and(me != g, g != last_group(chip)))
             def _():
                 send_end(ways[1], g).wait_send()
 
-    for k in range(1, nv):
-        c_copy(0, (v + k) % nv, v).wait_recv()
-    top, weight_sum, chosen = merge([shared[k] for k in range(nv)])
+    @pl.when(places[1] >= n - 2)
+    def _():
+        for k in range(nv):
+            @pl.when(jnp.logical_or(me != last_group(chip), v != k))
+            def _():
+                late_copy(0, k).wait_send()
+
+    for k in range(nv):
+        @pl.when(jnp.logical_and(last_group(k // 2) != me, v != k))
+        def _():
+            c_copy(0, k, v).wait_recv()
+
+        for e in range(len(ending)):
+            @pl.when(jnp.logical_and(last_group(k // 2) == me, jnp.logical_or(v != k, me != ending[e])))
+            def _():
+                late_arrival(k, e).wait_recv()
+
+    top, weight_sum, chosen = merge(
+        [shared[k] for k in range(nv)] + [late[k, e] for k in range(nv) for e in range(len(ending))]
+    )
     norm = top + jnp.log(weight_sum)
     for b, line in enumerate((norm, chosen)):
         for a in range(depths):
@@ -328,15 +420,17 @@
                 [line[:, (s * depths + a) * share : (s * depths + a + 1) * share] for s in range(2)], axis=1
             )
 
-    for k in range(1, nv):
-        c_copy(k - 1, v, (v + k) % nv).wait_send()
+    @pl.when(early)
+    def _():
+        for k in range(1, nv):
+            c_copy(k - 1, v, (v + k) % nv).wait_send()
 
 
 def body(n, nv, hidden, head_weight, targets):
     depths, share, width = hidden.shape
     columns = head_weight.shape[1]
     groups = nv // 2
-    assert groups == n and n >= 2 and depths * 2 * share == LANES
+    assert groups == n and n >= 4 and depths * 2 * share == LANES
     cw = min(512, columns // 2)
     nj = columns // 2 // cw
     units = nv * nj
@@ -354,10 +448,10 @@
         scratch_shapes=[
             pltpu.VMEM((groups, 2, depths, share, width), hidden.dtype),
             pltpu.VMEM((2 * nj, width, cw), head_weight.dtype),
-            pltpu.VMEM((2, units, block, cw), jnp.int16),
-            pltpu.VMEM((2, units, block, cw), jnp.int16),
-            pltpu.VMEM((2, units, 1, LANES), jnp.float32),
-            pltpu.VMEM((2, units, 1, LANES), jnp.float32),
+            pltpu.VMEM((2, units + BACK, block, cw), jnp.int16),
+            pltpu.VMEM((2, units + BACK, block, cw), jnp.int16),
+            pltpu.VMEM((2, units + BACK, 1, LANES), jnp.float32),
+            pltpu.VMEM((2, units + BACK, 1, LANES), jnp.float32),
             pltpu.VMEM((2, 2, block, cw), jnp.float32),
             pltpu.VMEM((n,) + targets.shape, jnp.int32),
             pltpu.VMEM((2 * block, LANES), jnp.int32),
@@ -367,9 +461,10 @@
             pltpu.VMEM((groups, 8, 2 * block), jnp.float32),
             pltpu.VMEM((2, 8, 2 * block), jnp.float32),
             pltpu.VMEM((nv, 8, 2 * block), jnp.float32),
-            dma((2 * nj,)), dma, dma, dma((nv,)), dma((2,)), dma((n,)),
+            pltpu.VMEM((nv, 4, 8, 2 * block), jnp.float32),
+            dma((2 * nj,)), dma, dma, dma((nv,)), dma((4,)), dma((n,)),
             dma((2,)), dma((2, ring)), dma((2,)), dma((2, ring)),
-            dma((groups,)), dma((2,)), dma((nv - 1,)), dma((nv,)),
+            dma((groups,)), dma((2,)), dma((nv - 1,)), dma((nv,)), dma, dma((nv, 4)),
         ],
         compiler_params=pltpu.CompilerParams(
             collective_id=0, has_side_effects=True, vmem_limit_bytes=60 * 1024 * 1024

time: 118 us -> 112 us (0.949)
  Pallas kernels: 115 us -> 110 us
    pallas_call x1, Pallas kernels: 115 us -> 110 us  [body(): pl.pallas_call(functools.partial(kernel, n, nv, nj, cw, ring), out_shape=...]
where the time goes in v1:
time: 112 us
  Pallas kernels  110 us (98%)
  other arithmetic  1.32 us (1%)
    pallas_call x1, Pallas kernels, body(): pl.pallas_call(functools.partial(kernel, n, nv, nj, cw, ring), out_shape=...  110 us

profile of v1, /device:TPU:0, one launch (start us, length us, event | category | flops | bytes accessed | tf_op | source)
XLA Modules:
  0.0 112.0 jit_solution(2410820573679885606)
XLA Ops:
  0.6 110.1 %shard_map.50 = f32[4,64]{1,0:T(4,128)} custom-call(bf16[2,32,1792]{2,1,0:T(8,128)(2,1)} %hidden.1, bf16[1792,8192]{1,0:T(8,128)(2,1)} %weight.1, s32[2,64]{1,0:T(2,128)} %targets.1), custom_call_target="tpu_custom_call" | custom-call | tf_op jit(solution)/shard_map/pallas_call | solution.py:443
  110.7 1.3 %slice_multiply_fusion = (f32[2,64]{1,0:T(2,128)}, f32[2,64]{1,0:T(2,128)}) fusion(f32[4,64]{1,0:T(4,128)} %shard_map.50), kind=kLoop, calls=%fused_computation.1 | loop fusion | flops 256 | bytes 2048 | tf_op jit(solution)/shard_map/mul | solution.py:474

commit v2 on v1

--- a/solution.py
+++ b/solution.py
@@ -22,7 +22,7 @@
     out,
     rows, wbuf, came, gone, came_scale, gone_scale, part,
     labels, label_tile, peak, mass, pick, ends, mine, shared, late,
-    w_sem, own_sem, h_send, h_recv, l_send, l_recv,
+    w_sem, own_sem, label_sem, h_send, h_recv, l_send, l_recv,
     q_send, q_recv, s_send, s_recv, e_send, e_recv, c_send, c_recv, t_send, t_recv,
 ):
     v, me = lax.axis_index("vocab"), lax.axis_index("hid")
@@ -50,7 +50,7 @@
         return pltpu.make_async_copy(
             weight.at[:, pl.ds(pl.multiple_of(ways[t] * half + j * cw, cw), cw)],
             wbuf.at[ways[t] * nj + j],
-            w_sem.at[t * nj + j],
+            w_sem.at[t, j % (AHEAD + 1)],
         )
 
     own = pltpu.make_async_copy(hidden, rows.at[chip, parity], own_sem)
@@ -60,8 +60,8 @@
     neutral = jnp.where(row == 0, LOWEST, 0.0)
     for k in range(nv):
         shared[k] = neutral
-        for e in range(len(ending)):
-            late[k, e] = neutral
+    for k in range(late.shape[0]):
+        late[k] = neutral
 
     barrier = pltpu.get_barrier_semaphore()
     for k in range(1, nv):
@@ -136,34 +136,13 @@
             def _():
                 big_dot(0, last_group(chip), ways[1] * nj + nj - 1)
 
-    own.wait()
-    w_copy(0, 0).wait()
-    small_dot(0, 0)
-    pl.semaphore_wait(barrier, nv - 1 + n - 1)
-
-    peers = [2 * chip + 1 - parity]
-    for back in range(1, groups):
-        other = (chip - back + groups) % groups
-        peers += [2 * other + parity, 2 * other + 1 - parity]
-    for target in peers:
-        h_copy(target).start()
-
     finals = (n - 1, 0)
 
     def l_copy(e):
         return pltpu.make_async_remote_copy(
-            src_ref=targets, dst_ref=labels.at[me], send_sem=l_send.at[e], recv_sem=l_recv.at[me],
+            src_ref=targets, dst_ref=labels.at[me], send_sem=l_send, recv_sem=l_recv,
             device_id=(v, ending[e]), device_id_type=MESH,
         )
-
-    for e in range(len(ending)):
-        @pl.when(me != ending[e])
-        def _():
-            l_copy(e).start()
-
-        @pl.when(me == ending[e])
-        def _():
-            labels[me] = targets[...]
 
     def message(t, u, target):
         way = ways[t]
@@ -181,7 +160,7 @@
 
     def send_end(e, g):
         return pltpu.make_async_remote_copy(
-            src_ref=ends.at[g], dst_ref=mine.at[e], send_sem=e_send.at[g], recv_sem=e_recv.at[e],
+            src_ref=ends.at[g], dst_ref=mine.at[e], send_sem=e_send, recv_sem=e_recv.at[e],
             device_id=(v, g), device_id_type=MESH,
         )
 
@@ -203,27 +182,59 @@
         scale = came_scale[ways[0], u]
         return [came[ways[0], u, :, c].astype(jnp.int32).astype(jnp.float32) * scale for c in columns]
 
+    def late_place(e):
+        return (chip // 2 * 2 + parity) * len(ending) + e
+
     def late_copy(e, target):
         return pltpu.make_async_remote_copy(
-            src_ref=ends.at[last_group(chip)], dst_ref=late.at[v, e], send_sem=t_send, recv_sem=t_recv.at[v, e],
+            src_ref=ends.at[last_group(chip)], dst_ref=late.at[late_place(e)], send_sem=t_send, recv_sem=t_recv,
             device_id=(target, last_group(chip)), device_id_type=MESH,
         )
 
-    def late_arrival(k, e):
-        return pltpu.make_async_remote_copy(
-            src_ref=ends.at[0], dst_ref=late.at[k, e], send_sem=t_send, recv_sem=t_recv.at[k, e],
-            device_id=(v, me), device_id_type=MESH,
-        )
-
-    def ship(t, u, pieces):
+    def prepare(t, u, pieces):
         largest = functools.reduce(jnp.maximum, [jnp.abs(piece) for piece in pieces])
         largest = jnp.maximum(jnp.max(largest, axis=0, keepdims=True), 1e-30)
         gone_scale[ways[t], u] = largest * (1.0 / TOP)
         up = TOP / largest
         for c, piece in zip(columns, pieces):
             gone[ways[t], u, :, c] = jnp.round(piece * up).astype(jnp.int32).astype(jnp.int16)
+
+    def launch(t, u):
         for copy in message(t, u, nexts[t]):
             copy.start()
+
+    def ship(t, u, pieces):
+        prepare(t, u, pieces)
+        launch(t, u)
+
+    own.wait()
+    w_copy(0, 0).wait()
+    small_dot(0, 0)
+
+    @pl.when(places[0] == 0)
+    def _():
+        prepare(0, 0, held(0, 0))
+
+    pl.semaphore_wait(barrier, nv - 1 + n - 1)
+
+    @pl.when(places[0] == 0)
+    def _():
+        launch(0, 0)
+
+    peers = [2 * chip + 1 - parity]
+    for back in range(1, groups):
+        other = (chip - back + groups) % groups
+        peers += [2 * other + parity, 2 * other + 1 - parity]
+    for target in peers:
+        h_copy(target).start()
+
+    for e in range(len(ending)):
+        @pl.when(me != ending[e])
+        def _():
+            l_copy(e).start()
+
+    own_labels = pltpu.make_async_copy(targets, labels.at[me], label_sem)
+    own_labels.start()
 
     def order(line):
         return jnp.concatenate(
@@ -235,13 +246,8 @@
 
         @pl.when(u == start)
         def _():
-            for z in range(n):
-                @pl.when(me != z)
-                def _():
-                    pltpu.make_async_remote_copy(
-                        src_ref=targets, dst_ref=labels.at[z], send_sem=l_send.at[0], recv_sem=l_recv.at[z],
-                        device_id=(v, me), device_id_type=MESH,
-                    ).wait_recv()
+            pltpu.make_async_copy(labels.at[0 : n - 1], labels.at[1:n], l_recv).wait()
+            pltpu.make_async_copy(targets, labels.at[me], label_sem).wait()
 
         @pl.when(jnp.logical_or(r == 0, u == start))
         def _():
@@ -282,7 +288,7 @@
                     def _():
                         @pl.when(me == last_group(chip))
                         def _():
-                            late[v, e] = ends[last_group(chip)]
+                            late[late_place(e)] = ends[last_group(chip)]
 
                         for k in range(nv):
                             @pl.when(jnp.logical_or(me != last_group(chip), v != k))
@@ -303,7 +309,7 @@
 
         @pl.when(jnp.logical_and(u >= 0, u < units + extra))
         def _():
-            @pl.when(places[0] == 0)
+            @pl.when(jnp.logical_and(places[0] == 0, u > 0))
             def _():
                 ship(0, u, held(0, u))
 
@@ -338,7 +344,8 @@
 
         return carry
 
-    lax.fori_loop(0, units + (n - 1) * SKEW, step, 0)
+    mine_last = jnp.where(places[1] == n - 1, kept, units)
+    lax.fori_loop(0, mine_last + places[1] * SKEW, step, 0)
 
     def merge(tiles):
         top = functools.reduce(jnp.maximum, [t[0:1] for t in tiles])
@@ -346,13 +353,15 @@
         chosen = sum(t[2:3] for t in tiles)
         return top, weight_sum, chosen
 
-    def c_copy(slot, source, target):
-        return pltpu.make_async_remote_copy(
-            src_ref=shared.at[source], dst_ref=shared.at[source], send_sem=c_send.at[slot], recv_sem=c_recv.at[source],
+    def c_copy(target):
+        return pltpu.make_async_remote_copy(
+            src_ref=shared.at[v], dst_ref=shared.at[v], send_sem=c_send, recv_sem=c_recv,
             device_id=(target, me), device_id_type=MESH,
         )
 
     early = last_group(chip) != me
+    at_end = functools.reduce(jnp.logical_or, [me == z for z in ending])
+    middle = jnp.logical_or(me == n // 2 - 1, me == n // 2)
 
     @pl.when(early)
     def _():
@@ -364,14 +373,17 @@
         top, weight_sum, chosen = merge([mine[0], mine[1]])
         shared[v] = jnp.concatenate([top, weight_sum, chosen, jnp.zeros((5, 2 * block), jnp.float32)], axis=0)
         for k in range(1, nv):
-            c_copy(k - 1, v, (v + k) % nv).start()
+            c_copy((v + k) % nv).start()
 
     for _ in range(nv - 1):
         h_copy(v).wait_send()
-    for e in range(len(ending)):
-        @pl.when(me != ending[e])
-        def _():
-            l_copy(e).wait_send()
+    def passed(ref, count, sem):
+        pltpu.make_async_copy(ref.at[0:count], ref.at[0:count], sem).wait()
+
+    for role, count in ((at_end, len(ending) - 1), (jnp.logical_not(at_end), len(ending))):
+        @pl.when(role)
+        def _():
+            passed(labels, count, l_send)
 
     def sent(t, count):
         way = ways[t]
@@ -388,30 +400,32 @@
 
     @pl.when(places[1] == n - 1)
     def _():
-        for g in range(groups):
-            @pl.when(jnp.logical_and(me != g, g != last_group(chip)))
-            def _():
-                send_end(ways[1], g).wait_send()
-
-    @pl.when(places[1] >= n - 2)
-    def _():
-        for k in range(nv):
-            @pl.when(jnp.logical_or(me != last_group(chip), v != k))
-            def _():
-                late_copy(0, k).wait_send()
-
-    for k in range(nv):
-        @pl.when(jnp.logical_and(last_group(k // 2) != me, v != k))
-        def _():
-            c_copy(0, k, v).wait_recv()
-
-        for e in range(len(ending)):
-            @pl.when(jnp.logical_and(last_group(k // 2) == me, jnp.logical_or(v != k, me != ending[e])))
-            def _():
-                late_arrival(k, e).wait_recv()
+        passed(ends, groups - 2, e_send)
+
+    for role, count in ((early, nv), (jnp.logical_not(early), nv - 1)):
+        @pl.when(jnp.logical_and(role, places[1] >= n - 2))
+        def _():
+            passed(late, count, t_send)
+
+    for role, count in (
+        (jnp.logical_not(middle), nv - 1),
+        (jnp.logical_and(middle, early), nv // 2 - 1),
+        (jnp.logical_not(early), nv // 2),
+    ):
+        @pl.when(role)
+        def _():
+            passed(shared, count, c_recv)
+
+    for role, count in (
+        (jnp.logical_and(middle, jnp.logical_or(early, jnp.logical_not(at_end))), late.shape[0]),
+        (jnp.logical_and(jnp.logical_not(early), at_end), late.shape[0] - 1),
+    ):
+        @pl.when(role)
+        def _():
+            passed(late, count, t_recv)
 
     top, weight_sum, chosen = merge(
-        [shared[k] for k in range(nv)] + [late[k, e] for k in range(nv) for e in range(len(ending))]
+        [shared[k] for k in range(nv)] + [late[k] for k in range(late.shape[0])]
     )
     norm = top + jnp.log(weight_sum)
     for b, line in enumerate((norm, chosen)):
@@ -422,8 +436,7 @@
 
     @pl.when(early)
     def _():
-        for k in range(1, nv):
-            c_copy(k - 1, v, (v + k) % nv).wait_send()
+        passed(shared, nv - 1, c_send)
 
 
 def body(n, nv, hidden, head_weight, targets):
@@ -443,7 +456,7 @@
     result = pl.pallas_call(
         functools.partial(kernel, n, nv, nj, cw, ring),
         out_shape=jax.ShapeDtypeStruct((2 * depths, targets.shape[1]), jnp.float32),
-        in_specs=[anywhere, anywhere, vmem],
+        in_specs=[anywhere, anywhere, anywhere],
         out_specs=vmem,
         scratch_shapes=[
             pltpu.VMEM((groups, 2, depths, share, width), hidden.dtype),
@@ -461,10 +474,10 @@
             pltpu.VMEM((groups, 8, 2 * block), jnp.float32),
             pltpu.VMEM((2, 8, 2 * block), jnp.float32),
             pltpu.VMEM((nv, 8, 2 * block), jnp.float32),
-            pltpu.VMEM((nv, 4, 8, 2 * block), jnp.float32),
-            dma((2 * nj,)), dma, dma, dma((nv,)), dma((4,)), dma((n,)),
+            pltpu.VMEM((2 * nv, 8, 2 * block), jnp.float32),
+            dma((2, AHEAD + 1)), dma, dma, dma, dma((nv,)), dma, dma,
             dma((2,)), dma((2, ring)), dma((2,)), dma((2, ring)),
-            dma((groups,)), dma((2,)), dma((nv - 1,)), dma((nv,)), dma, dma((nv, 4)),
+            dma, dma((2,)), dma, dma, dma, dma,
         ],
         compiler_params=pltpu.CompilerParams(
             collective_id=0, has_side_effects=True, vmem_limit_bytes=60 * 1024 * 1024

time: 112 us -> 111 us (level)
    pallas_call x1, Pallas kernels: 110 us -> 109 us  [body(): pl.pallas_call(functools.partial(kernel, n, nv, nj, cw, ring), out_shape=...]
where the time goes in v2:
time: 111 us
  Pallas kernels  109 us (98%)
  other arithmetic  1.32 us (1%)
    pallas_call x1, Pallas kernels, body(): pl.pallas_call(functools.partial(kernel, n, nv, nj, cw, ring), out_shape=...  109 us

profile of v2, /device:TPU:0, one launch (start us, length us, event | category | flops | bytes accessed | tf_op | source)
XLA Modules:
  0.0 110.6 jit_solution(6719645022451059698)
XLA Ops:
  0.6 108.7 %shard_map.50 = f32[4,64]{1,0:T(4,128)} custom-call(bf16[2,32,1792]{2,1,0:T(8,128)(2,1)} %hidden.1, bf16[1792,8192]{1,0:T(8,128)(2,1)} %weight.1, s32[2,64]{1,0:T(2,128)} %targets.1), custom_call_target="tpu_custom_call" | custom-call | tf_op jit(solution)/shard_map/pallas_call | solution.py:456
  109.3 1.3 %slice_multiply_fusion = (f32[2,64]{1,0:T(2,128)}, f32[2,64]{1,0:T(2,128)}) fusion(f32[4,64]{1,0:T(4,128)} %shard_map.50), kind=kLoop, calls=%fused_computation.1 | loop fusion | flops 256 | bytes 2048 | tf_op jit(solution)/shard_map/mul | solution.py:487

commit v3 on v2

--- a/solution.py
+++ b/solution.py
@@ -11,7 +11,7 @@
 LANES = 128
 SKEW = 3
 AHEAD = 3
-BACK = 2
+BACK = 3
 LOWEST = -3.0e38
 TOP = 32767.0
 
@@ -69,11 +69,6 @@
     for k in range(1, n):
         pl.semaphore_signal(barrier, inc=1, device_id=(v, (me + k) % n), device_id_type=MESH)
 
-    for j in range(1, AHEAD):
-        w_copy(0, j).start()
-    for j in range(AHEAD - 1):
-        w_copy(1, j).start()
-
     def h_copy(target):
         return pltpu.make_async_remote_copy(
             src_ref=hidden, dst_ref=rows.at[chip, parity], send_sem=h_send, recv_sem=h_recv.at[v],
@@ -132,9 +127,12 @@
             big_dot(t, g, ways[t] * nj + (u % span) // 2)
 
         if t == 0:
-            @pl.when(jnp.logical_and(u == units, places[0] == 0))
-            def _():
-                big_dot(0, last_group(chip), ways[1] * nj + nj - 1)
+            @pl.when(u >= units)
+            def _():
+                back = u - BACK
+                a = rows[last_group(chip), back % 2].reshape(block, width)
+                chunk = ways[1] * nj + (back % span) // 2
+                part[0, u % 2] = jnp.dot(a, wbuf[chunk], preferred_element_type=jnp.float32)
 
     finals = (n - 1, 0)
 
@@ -209,6 +207,11 @@
 
     own.wait()
     w_copy(0, 0).wait()
+    for j in range(1, AHEAD):
+        w_copy(0, j).start()
+    for j in range(AHEAD - 1):
+        w_copy(1, j).start()
+
     small_dot(0, 0)
 
     @pl.when(places[0] == 0)
@@ -303,50 +306,6 @@
             def _():
                 mine[ways[1]] = ends[g]
 
-    def step(i, carry):
-        u = i - places[0] * SKEW
-        extra = jnp.where(places[0] == 0, BACK, 0)
-
-        @pl.when(jnp.logical_and(u >= 0, u < units + extra))
-        def _():
-            @pl.when(jnp.logical_and(places[0] == 0, u > 0))
-            def _():
-                ship(0, u, held(0, u))
-
-            @pl.when(places[0] > 0)
-            def _():
-                ship(0, u, received(0, u))
-
-        w = i - places[1] * SKEW
-
-        @pl.when(jnp.logical_and(w >= 0, w < units))
-        def _():
-            @pl.when(jnp.logical_and(places[1] < n - 1, jnp.logical_or(w < kept, places[1] < n - 2)))
-            def _():
-                ship(1, w, received(1, w))
-
-            @pl.when(jnp.logical_and(places[1] == n - 1, w < kept))
-            def _():
-                statistics(w, received(1, w), 0, kept)
-
-            @pl.when(jnp.logical_and(places[1] == n - 2, w >= kept))
-            def _():
-                total = [a + b for a, b in zip(received(1, w), returned(w + BACK))]
-                statistics(w, total, kept, units)
-
-        @pl.when(jnp.logical_and(u >= 0, u < units))
-        def _():
-            dot(0, u + 1)
-
-        @pl.when(jnp.logical_and(w >= -1, w < jnp.where(places[1] == n - 1, kept, units) - 1))
-        def _():
-            dot(1, w + 1)
-
-        return carry
-
-    mine_last = jnp.where(places[1] == n - 1, kept, units)
-    lax.fori_loop(0, mine_last + places[1] * SKEW, step, 0)
-
     def merge(tiles):
         top = functools.reduce(jnp.maximum, [t[0:1] for t in tiles])
         weight_sum = sum(t[1:2] * jnp.exp(t[0:1] - top) for t in tiles)
@@ -363,8 +322,7 @@
     at_end = functools.reduce(jnp.logical_or, [me == z for z in ending])
     middle = jnp.logical_or(me == n // 2 - 1, me == n // 2)
 
-    @pl.when(early)
-    def _():
+    def exchange():
         for e in range(2):
             @pl.when(me != finals[e])
             def _():
@@ -375,37 +333,56 @@
         for k in range(1, nv):
             c_copy((v + k) % nv).start()
 
-    for _ in range(nv - 1):
-        h_copy(v).wait_send()
     def passed(ref, count, sem):
         pltpu.make_async_copy(ref.at[0:count], ref.at[0:count], sem).wait()
 
-    for role, count in ((at_end, len(ending) - 1), (jnp.logical_not(at_end), len(ending))):
-        @pl.when(role)
-        def _():
-            passed(labels, count, l_send)
-
-    def sent(t, count):
-        way = ways[t]
-        pltpu.make_async_copy(gone.at[way, 0:count], came.at[way, 0:count], q_send.at[way]).wait()
-        pltpu.make_async_copy(gone_scale.at[way, 0:count], came_scale.at[way, 0:count], s_send.at[way]).wait()
-
-    for t, role, count in (
-        (0, places[0] == 0, units + BACK), (0, places[0] > 0, units),
-        (1, places[1] < n - 2, units), (1, places[1] == n - 2, kept),
-    ):
-        @pl.when(role)
-        def _():
-            sent(t, count)
-
-    @pl.when(places[1] == n - 1)
-    def _():
-        passed(ends, groups - 2, e_send)
-
-    for role, count in ((early, nv), (jnp.logical_not(early), nv - 1)):
-        @pl.when(jnp.logical_and(role, places[1] >= n - 2))
-        def _():
-            passed(late, count, t_send)
+    def step(i, carry):
+        u = i - places[0] * SKEW
+        extra = jnp.where(places[0] == 0, BACK, 0)
+
+        @pl.when(jnp.logical_and(u >= 0, u < units + extra))
+        def _():
+            @pl.when(jnp.logical_and(places[0] == 0, u > 0))
+            def _():
+                ship(0, u, held(0, u))
+
+            @pl.when(places[0] > 0)
+            def _():
+                ship(0, u, received(0, u))
+
+        w = i - places[1] * SKEW
+
+        @pl.when(jnp.logical_and(w >= 0, w < units))
+        def _():
+            @pl.when(jnp.logical_and(places[1] < n - 1, jnp.logical_or(w < kept, places[1] < n - 2)))
+            def _():
+                ship(1, w, received(1, w))
+
+            @pl.when(jnp.logical_and(places[1] == n - 1, w < kept))
+            def _():
+                statistics(w, received(1, w), 0, kept)
+
+            @pl.when(jnp.logical_and(places[1] == n - 2, w >= kept))
+            def _():
+                total = [a + b for a, b in zip(received(1, w), returned(w + BACK))]
+                statistics(w, total, kept, units)
+
+        @pl.when(jnp.logical_and(u >= 0, u < units + extra - 1))
+        def _():
+            dot(0, u + 1)
+
+        @pl.when(jnp.logical_and(w == units - nj, early))
+        def _():
+            exchange()
+
+        @pl.when(jnp.logical_and(w >= -1, w < jnp.where(places[1] == n - 1, kept, units) - 1))
+        def _():
+            dot(1, w + 1)
+
+        return carry
+
+    mine_last = jnp.where(places[1] == n - 1, kept, units)
+    lax.fori_loop(0, mine_last + places[1] * SKEW, step, 0)
 
     for role, count in (
         (jnp.logical_not(middle), nv - 1),
@@ -424,15 +401,51 @@
         def _():
             passed(late, count, t_recv)
 
-    top, weight_sum, chosen = merge(
-        [shared[k] for k in range(nv)] + [late[k] for k in range(late.shape[0])]
-    )
-    norm = top + jnp.log(weight_sum)
-    for b, line in enumerate((norm, chosen)):
-        for a in range(depths):
-            out[depths * b + a : depths * b + a + 1, :] = jnp.concatenate(
-                [line[:, (s * depths + a) * share : (s * depths + a + 1) * share] for s in range(2)], axis=1
-            )
+    def finish(tiles):
+        top, weight_sum, chosen = merge(tiles)
+        norm = top + jnp.log(weight_sum)
+        for b, line in enumerate((norm, chosen)):
+            for a in range(depths):
+                out[depths * b + a : depths * b + a + 1, :] = jnp.concatenate(
+                    [line[:, (s * depths + a) * share : (s * depths + a + 1) * share] for s in range(2)], axis=1
+                )
+
+    @pl.when(middle)
+    def _():
+        finish([shared[k] for k in range(nv)] + [late[k] for k in range(late.shape[0])])
+
+    @pl.when(jnp.logical_not(middle))
+    def _():
+        finish([shared[k] for k in range(nv)])
+
+    for _ in range(nv - 1):
+        h_copy(v).wait_send()
+    for role, count in ((at_end, len(ending) - 1), (jnp.logical_not(at_end), len(ending))):
+        @pl.when(role)
+        def _():
+            passed(labels, count, l_send)
+
+    def sent(t, count):
+        way = ways[t]
+        pltpu.make_async_copy(gone.at[way, 0:count], came.at[way, 0:count], q_send.at[way]).wait()
+        pltpu.make_async_copy(gone_scale.at[way, 0:count], came_scale.at[way, 0:count], s_send.at[way]).wait()
+
+    for t, role, count in (
+        (0, places[0] == 0, units + BACK), (0, places[0] > 0, units),
+        (1, places[1] < n - 2, units), (1, places[1] == n - 2, kept),
+    ):
+        @pl.when(role)
+        def _():
+            sent(t, count)
+
+    @pl.when(places[1] == n - 1)
+    def _():
+        passed(ends, groups - 2, e_send)
+
+    for role, count in ((early, nv), (jnp.logical_not(early), nv - 1)):
+        @pl.when(jnp.logical_and(role, places[1] >= n - 2))
+        def _():
+            passed(late, count, t_send)
 
     @pl.when(early)
     def _():

time: 111 us -> 109 us (0.982); the launches traced: 111 us -> 107 us
  Pallas kernels: 109 us -> 105 us
    pallas_call x1, Pallas kernels: 109 us -> 105 us  [body(): pl.pallas_call(functools.partial(kernel, n, nv, nj, cw, ring), out_shape=...]
where the time goes in v3:
time: 109 us; the launch traced here: 107 us
  Pallas kernels  105 us (96%)
  other arithmetic  1.32 us (1%)
    pallas_call x1, Pallas kernels, body(): pl.pallas_call(functools.partial(kernel, n, nv, nj, cw, ring), out_shape=...  105 us

profile of v3, /device:TPU:0, one launch (start us, length us, event | category | flops | bytes accessed | tf_op | source)
XLA Modules:
  0.0 107.4 jit_solution(6368723555359729713)
XLA Ops:
  0.6 105.5 %shard_map.50 = f32[4,64]{1,0:T(4,128)} custom-call(bf16[2,32,1792]{2,1,0:T(8,128)(2,1)} %hidden.1, bf16[1792,8192]{1,0:T(8,128)(2,1)} %weight.1, s32[2,64]{1,0:T(2,128)} %targets.1), custom_call_target="tpu_custom_call" | custom-call | tf_op jit(solution)/shard_map/pallas_call | solution.py:469
  106.1 1.3 %slice_multiply_fusion = (f32[2,64]{1,0:T(2,128)}, f32[2,64]{1,0:T(2,128)}) fusion(f32[4,64]{1,0:T(4,128)} %shard_map.50), kind=kLoop, calls=%fused_computation.1 | loop fusion | flops 256 | bytes 2048 | tf_op jit(solution)/shard_map/mul | solution.py:500

commit v4 on v3

--- a/solution.py
+++ b/solution.py
@@ -56,7 +56,7 @@
     own = pltpu.make_async_copy(hidden, rows.at[chip, parity], own_sem)
     own.start()
     w_copy(0, 0).start()
-    row = lax.broadcasted_iota(jnp.int32, (8, 2 * block), 0)
+    row = lax.broadcasted_iota(jnp.int32, (4, 2 * block), 0)
     neutral = jnp.where(row == 0, LOWEST, 0.0)
     for k in range(nv):
         shared[k] = neutral
@@ -281,7 +281,7 @@
             weight_sum = jnp.sum(jnp.transpose(mass[...]) * jnp.exp(tall - top), axis=0, keepdims=True)
             chosen = jnp.sum(jnp.transpose(pick[...]), axis=0, keepdims=True)
             ends[g] = jnp.concatenate(
-                [top, weight_sum, chosen, jnp.zeros((5, 2 * block), jnp.float32)], axis=0
+                [top, weight_sum, chosen, jnp.zeros((1, 2 * block), jnp.float32)], axis=0
             )
 
             @pl.when(u == stop - 1)
@@ -307,9 +307,14 @@
                 mine[ways[1]] = ends[g]
 
     def merge(tiles):
-        top = functools.reduce(jnp.maximum, [t[0:1] for t in tiles])
-        weight_sum = sum(t[1:2] * jnp.exp(t[0:1] - top) for t in tiles)
-        chosen = sum(t[2:3] for t in tiles)
+        def pairwise(join, terms):
+            while len(terms) > 1:
+                terms = [join(*terms[k : k + 2]) if k + 1 < len(terms) else terms[k] for k in range(0, len(terms), 2)]
+            return terms[0]
+
+        top = pairwise(jnp.maximum, [t[0:1] for t in tiles])
+        weight_sum = pairwise(jnp.add, [t[1:2] * jnp.exp(t[0:1] - top) for t in tiles])
+        chosen = pairwise(jnp.add, [t[2:3] for t in tiles])
         return top, weight_sum, chosen
 
     def c_copy(target):
@@ -329,7 +334,7 @@
                 send_end(e, me).wait_recv()
 
         top, weight_sum, chosen = merge([mine[0], mine[1]])
-        shared[v] = jnp.concatenate([top, weight_sum, chosen, jnp.zeros((5, 2 * block), jnp.float32)], axis=0)
+        shared[v] = jnp.concatenate([top, weight_sum, chosen, jnp.zeros((1, 2 * block), jnp.float32)], axis=0)
         for k in range(1, nv):
             c_copy((v + k) % nv).start()
 
@@ -484,10 +489,10 @@
             pltpu.VMEM((2 * block, LANES), jnp.float32),
             pltpu.VMEM((2 * block, LANES), jnp.float32),
             pltpu.VMEM((2 * block, LANES), jnp.float32),
-            pltpu.VMEM((groups, 8, 2 * block), jnp.float32),
-            pltpu.VMEM((2, 8, 2 * block), jnp.float32),
-            pltpu.VMEM((nv, 8, 2 * block), jnp.float32),
-            pltpu.VMEM((2 * nv, 8, 2 * block), jnp.float32),
+            pltpu.VMEM((groups, 4, 2 * block), jnp.float32),
+            pltpu.VMEM((2, 4, 2 * block), jnp.float32),
+            pltpu.VMEM((nv, 4, 2 * block), jnp.float32),
+            pltpu.VMEM((2 * nv, 4, 2 * block), jnp.float32),
             dma((2, AHEAD + 1)), dma, dma, dma, dma((nv,)), dma, dma,
             dma((2,)), dma((2, ring)), dma((2,)), dma((2, ring)),
             dma, dma((2,)), dma, dma, dma, dma,

time: 109 us -> 108 us (level)
  no operation moved by 1% of the time
where the time goes in v4:
time: 108 us; the launch traced here: 107 us
  Pallas kernels  105 us (97%)
  other arithmetic  1.32 us (1%)
    pallas_call x1, Pallas kernels, body(): pl.pallas_call(functools.partial(kernel, n, nv, nj, cw, ring), out_shape=...  105 us

profile of v4, /device:TPU:0, one launch (start us, length us, event | category | flops | bytes accessed | tf_op | source)
XLA Modules:
  0.0 107.2 jit_solution(15164528205142309600)
XLA Ops:
  0.6 105.2 %shard_map.50 = f32[4,64]{1,0:T(4,128)} custom-call(bf16[2,32,1792]{2,1,0:T(8,128)(2,1)} %hidden.1, bf16[1792,8192]{1,0:T(8,128)(2,1)} %weight.1, s32[2,64]{1,0:T(2,128)} %targets.1), custom_call_target="tpu_custom_call" | custom-call | tf_op jit(solution)/shard_map/pallas_call | solution.py:474
  105.9 1.3 %slice_multiply_fusion = (f32[2,64]{1,0:T(2,128)}, f32[2,64]{1,0:T(2,128)}) fusion(f32[4,64]{1,0:T(4,128)} %shard_map.50), kind=kLoop, calls=%fused_computation.1 | loop fusion | flops 256 | bytes 2048 | tf_op jit(solution)/shard_map/mul | solution.py:505
